TPU v7x, 32 devices: a whole 2x2x4 slice. The times are simulated.
32 devices in a mesh: fine: 8 (over z, core), sub: 2 (over x), dp: 2 (over y).
Axes of the slice: x: 2, y: 2, z: 4, core: 2. Of those that a mesh axis runs over, the one named last changes fastest.
Arguments:
- queries: bfloat16 [2, 1024, 512], P('dp', 'fine', 'sub'), may hold values from -6 to 6
- keys: bfloat16 [2, 1024, 512], P('dp', 'fine', 'sub'), may hold values from -6 to 6
- values: bfloat16 [2, 1024, 512], P('dp', 'fine', 'sub'), may hold values from -6 to 6
- out_grad: bfloat16 [2, 1024, 512], P('dp', 'fine', 'sub'), may hold values from -6 to 6
- coarse_keys: bfloat16 [2, 512, 512], P(None, ('fine', 'sub', 'dp')), may hold values from -6 to 6
- coarse_values: bfloat16 [2, 512, 512], P(None, ('fine', 'sub', 'dp')), may hold values from -6 to 6
- fine_scale: int32 [1024], replicated, may hold values from 0 to 2, never falling along the last dimension, each value on 1 to 640 neighbouring positions
Outputs:
- attended: bfloat16 [2, 1024, 512], P('dp', 'fine', 'sub')
- query_grad: bfloat16 [2, 1024, 512], P('dp', 'fine', 'sub')
- key_grad: bfloat16 [2, 1024, 512], P('dp', 'fine', 'sub')
- value_grad: bfloat16 [2, 1024, 512], P('dp', 'fine', 'sub')
- coarse_key_grad: bfloat16 [2, 512, 512], P(None, ('fine', 'sub', 'dp'))
- coarse_value_grad: bfloat16 [2, 512, 512], P(None, ('fine', 'sub', 'dp'))
Inputs may be any that keep to these rules, and one draw needn't show every extreme that they name: `fine_scale`: the scale of each fine token among the last three scales, numbered from 0; it never falls along the tokens and every scale holds at least one token.
All inputs are finite; a program needn't handle non-finite values.
Results may differ from a plain program's by a relative error of at most 0.0098.
Values may be sent and summed in bfloat16 or wider, within the bound.
A program may use at most 64 MiB of HBM per device.

v0:
```python
import functools
import math

import jax
import jax.numpy as jnp
from jax import lax
from jax.experimental import pallas as pl
from jax.experimental.pallas import tpu as pltpu
from jax.sharding import PartitionSpec as P

HEAD = 128
CORES = 2
MESH = pl.DeviceIdType.MESH
INVERSE = 1.0 / math.sqrt(HEAD)


def nt(a, b):
    return lax.dot_general(a, b, (((1,), (1,)), ((), ())), preferred_element_type=jnp.float32)


def nn(a, b):
    return jnp.dot(a, b, preferred_element_type=jnp.float32)


def wait_bytes(ref, sem):
    pltpu.make_async_copy(ref, ref, sem).wait()


def kernel(
    sizes,
    direct,
    queries,
    keys,
    values,
    out_grad,
    coarse_keys,
    coarse_values,
    scale_in,
    attended,
    query_grad,
    key_grad,
    value_grad,
    coarse_key_grad,
    coarse_value_grad,
    scale_row,
    kv_src,
    qg_src,
    c_src,
    kv,
    qg,
    ckv,
    stats,
    stage,
    coarse_stage,
    key_acc,
    value_acc,
    load_sem,
    kv_recv,
    c_recv,
    qg_recv,
    stat_recv,
    out_recv,
    cg_recv,
    kv_send,
    c_send,
    qg_send,
    near_send,
    stat_send,
    out_send,
    cg_send,
):
    n_fine, n_sub, n_dp = sizes
    fine, sub, dp = lax.axis_index("fine"), lax.axis_index("sub"), lax.axis_index("dp")
    chip, core = fine // CORES, lax.rem(fine, CORES)
    chips = n_fine // CORES
    rows = keys.shape[1]
    span = rows * CORES
    coarse_rows = ckv.shape[1]
    coarse_span = coarse_rows // chips
    partner = {"fine": chip * CORES + (1 - core)}

    loads = []
    for slot, (src, dst) in enumerate(
        (
            (keys.at[0], kv_src.at[0]),
            (values.at[0], kv_src.at[1]),
            (coarse_keys, c_src.at[0]),
            (coarse_values, c_src.at[1]),
            (queries.at[0], qg_src.at[0]),
            (out_grad.at[0], qg_src.at[1]),
            (scale_in, scale_row),
        )
    ):
        copy = pltpu.make_async_copy(src, dst, load_sem.at[slot])
        copy.start()
        loads.append(copy)

    barrier = pltpu.get_barrier_semaphore()
    plane = []
    for step_core in range(CORES):
        for step_sub in range(n_sub if direct else 1):
            for step_dp in range(n_dp if direct else 1):
                if step_core or step_sub or step_dp:
                    plane.append(
                        (
                            chip * CORES + lax.rem(core + step_core, CORES),
                            lax.rem(sub + step_sub, n_sub),
                            lax.rem(dp + step_dp, n_dp),
                        )
                    )
    column = []
    for step_chip in range(1, chips):
        for step_core in range(CORES):
            to_chip = lax.rem(chip + step_chip, chips)
            column.append((to_chip * CORES + lax.rem(core + step_core, CORES), sub, dp))
    for other in column + plane:
        pl.semaphore_signal(barrier, inc=1, device_id=other, device_id_type=MESH)
    pl.semaphore_wait(barrier, len(column + plane))

    def head_columns(index):
        return pl.ds(pl.multiple_of(index * HEAD, HEAD), HEAD)

    my_rows = pl.ds(pl.multiple_of(fine * rows, rows), rows)
    chip_rows = pl.ds(pl.multiple_of(chip * span, span), span)
    chip_coarse = pl.ds(pl.multiple_of(chip * coarse_span, coarse_span), coarse_span)

    def remote(src, dst, send, recv, device):
        pltpu.make_async_remote_copy(
            src_ref=src,
            dst_ref=dst,
            send_sem=send,
            recv_sem=recv,
            device_id=device,
            device_id_type=MESH,
        ).start()

    def towards(right, act):
        to = chip + 1 if right else chip - 1
        pl.when(to < chips if right else to >= 0)(lambda: act(to))

    def send_own(src, dst, send, recv, right):
        def both_cores(to):
            for to_core in range(CORES):
                remote(
                    src.at[:, :, to_core * HEAD : (to_core + 1) * HEAD],
                    dst.at[:, my_rows],
                    send.at[right, 0],
                    recv.at[chip],
                    {"fine": to * CORES + to_core},
                )

        towards(right, both_cores)

    def share(src, dst, near, recv):
        remote(
            src.at[:, :, head_columns(1 - core)], dst.at[:, my_rows], near, recv.at[chip], partner
        )
        pltpu.make_async_copy(
            src.at[:, :, head_columns(core)], dst.at[:, my_rows], recv.at[chip]
        ).start()

    def block_of(at, size):
        return pl.ds(pl.multiple_of(at * size, size), size)

    def pass_on(buffer, size, send, recv, hop, right):
        at = chip - hop if right else chip + hop

        def arrived(to):
            block = buffer.at[:, block_of(at, size)]
            wait_bytes(block, recv.at[at])
            remote(block, block, send.at[right, hop], recv.at[at], {"fine": to * CORES + core})

        pl.when(at >= 0 if right else at < chips)(lambda: towards(right, arrived))

    loads[0].wait()
    loads[1].wait()
    for right in (0, 1):
        send_own(kv_src, kv, kv_send, kv_recv, right)
    share(kv_src, kv, near_send.at[0], kv_recv)
    loads[2].wait()
    loads[3].wait()
    mine = coarse_keys.shape[1]
    if direct:
        block = (fine * n_sub + sub) * n_dp + dp
    else:
        block = fine
    mine_rows = pl.ds(pl.multiple_of(block * mine, mine), mine)

    def coarse_piece(image, index):
        return c_src.at[:, image, :, head_columns(index)]

    for to_fine, to_sub, to_dp in plane:
        to_core = lax.rem(to_fine, CORES)
        piece = coarse_piece(to_dp, to_sub * CORES + to_core) if direct else coarse_piece(0, to_core)
        remote(piece, ckv.at[:, mine_rows], near_send.at[2], c_recv.at[chip], (to_fine, to_sub, to_dp))
    piece = coarse_piece(dp, sub * CORES + core) if direct else coarse_piece(0, core)
    pltpu.make_async_copy(piece, ckv.at[:, mine_rows], c_recv.at[chip]).start()
    loads[4].wait()
    loads[5].wait()
    share(qg_src, qg, near_send.at[1], qg_recv)

    own_coarse = ckv.at[:, chip_coarse]
    wait_bytes(own_coarse, c_recv.at[chip])
    for right in (0, 1):
        towards(
            right,
            lambda to, right=right: remote(
                own_coarse,
                own_coarse,
                c_send.at[right, 0],
                c_recv.at[chip],
                {"fine": to * CORES + core},
            ),
        )
    at_end = jnp.logical_or(chip == 0, chip == chips - 1)
    for hop in range(1, chips):
        for right in (0, 1):
            pass_on(kv, span, kv_send, kv_recv, hop, right)
            pass_on(ckv, coarse_span, c_send, c_recv, hop, right)
            spent = chip == hop - 1 if right else chip == chips - hop
            pl.when(spent)(
                lambda right=right: send_own(qg_src, qg, qg_send, qg_recv, right)
            )
    if chips > 2:
        for right in (0, 1):
            pass_on(qg, span, qg_send, qg_recv, 1, right)
    for step in range(1, chips):
        at = lax.rem(chip + step, chips)

        def last_stop(at=at):
            wait_bytes(kv.at[:, block_of(at, span)], kv_recv.at[at])
            wait_bytes(ckv.at[:, block_of(at, coarse_span)], c_recv.at[at])

        pl.when(at_end)(last_stop)

    loads[6].wait()
    scales = scale_row[...].astype(jnp.float32)
    own_scale = scale_row[:, chip_rows].astype(jnp.float32)
    own_column = jnp.transpose(jnp.broadcast_to(own_scale, (HEAD, span)))[:, :1]

    wait_bytes(qg.at[:, chip_rows], qg_recv.at[chip])
    query_own, grad_own = qg[0, chip_rows], qg[1, chip_rows]
    wait_bytes(kv.at[:, chip_rows], kv_recv.at[chip])
    fine_scores = nt(query_own, kv[0]) * INVERSE
    fine_scores = jnp.where(scales <= own_column, fine_scores, -jnp.inf)
    coarse_scores = nt(query_own, ckv[0]) * INVERSE
    peak = jnp.maximum(
        jnp.max(fine_scores, axis=1, keepdims=True), jnp.max(coarse_scores, axis=1, keepdims=True)
    )
    total = jnp.sum(jnp.exp(fine_scores - peak), axis=1, keepdims=True) + jnp.sum(
        jnp.exp(coarse_scores - peak), axis=1, keepdims=True
    )
    log_total = peak + jnp.log(total)
    fine_weights = jnp.exp(fine_scores - log_total).astype(jnp.bfloat16)
    coarse_weights = jnp.exp(coarse_scores - log_total).astype(jnp.bfloat16)
    for hop in range(2, chips - 1):
        for right in (0, 1):
            pass_on(qg, span, qg_send, qg_recv, hop, right)
    out = (nn(fine_weights, kv[1]) + nn(coarse_weights, ckv[1])).astype(jnp.bfloat16)
    delta = jnp.sum(
        grad_own.astype(jnp.float32) * out.astype(jnp.float32), axis=1, keepdims=True
    )
    log_rows = jnp.transpose(jnp.broadcast_to(log_total, (span, HEAD)))[:8]
    delta_rows = jnp.transpose(jnp.broadcast_to(delta, (span, HEAD)))[:8]
    first = lax.broadcasted_iota(jnp.int32, (8, span), 0) == 0
    stats[chip] = jnp.where(first, log_rows, delta_rows)
    for step in range(1, chips):
        to = lax.rem(chip + step, chips)
        remote(
            stats.at[chip],
            stats.at[chip],
            stat_send,
            stat_recv.at[chip],
            {"fine": to * CORES + core},
        )

    def hand_out(slot, value, result):
        height = value.shape[0] // CORES
        stage[slot, : value.shape[0]] = value
        give = pl.ds(pl.multiple_of((1 - core) * height, height), height)
        keep = pl.ds(pl.multiple_of(core * height, height), height)
        remote(
            stage.at[slot, give],
            result.at[0, :, head_columns(core)],
            out_send.at[slot],
            out_recv.at[slot],
            partner,
        )
        result[0, :, head_columns(core)] = stage[slot, keep]

    def collect(slot, result):
        half = result.at[0, :, head_columns(1 - core)]
        wait_bytes(half, out_recv.at[slot])
        wait_bytes(half, out_send.at[slot])

    hand_out(0, out, attended)

    def grads_of(weights, dots, row_delta):
        return (weights.astype(jnp.float32) * (dots - row_delta) * INVERSE).astype(jnp.bfloat16)

    fine_grads = grads_of(fine_weights, nt(grad_own, kv[1]), delta)
    coarse_grads = grads_of(coarse_weights, nt(grad_own, ckv[1]), delta)
    query_out = nn(fine_grads, kv[0]) + nn(coarse_grads, ckv[0])
    hand_out(1, query_out.astype(jnp.bfloat16), query_grad)

    reach = jnp.minimum(chip, chips - 1 - chip)
    longer = jnp.where(chip > chips - 1 - chip, -1, 1)
    for step in range(chips):
        near = -(step + 1) // 2 if step % 2 else step // 2
        at = chip + jnp.where(step <= 2 * reach, near, longer * (step - reach))
        at_rows = pl.ds(pl.multiple_of(at * span, span), span)
        if step:

            def last_queries(at=at, at_rows=at_rows):
                wait_bytes(qg.at[:, at_rows], qg_recv.at[at])

            pl.when(at_end)(last_queries)
            wait_bytes(stats.at[at], stat_recv.at[at])
        query_block, grad_block = qg[0, at_rows], qg[1, at_rows]
        log_row, delta_row = stats[at, 0:1], stats[at, 1:2]
        block_scale = scale_row[:, at_rows].astype(jnp.float32)
        for part in range(2):
            source, own, low = ((kv, chip_rows, 0), (ckv, chip_coarse, span))[part]
            high = low + (span, coarse_span)[part]
            scores = nt(source[0, own], query_block) * INVERSE
            if part == 0:
                scores = jnp.where(own_column <= block_scale, scores, -jnp.inf)
            weights = jnp.exp(scores - log_row).astype(jnp.bfloat16)
            value_part = nn(weights, grad_block)
            grads = grads_of(weights, nt(source[1, own], grad_block), delta_row)
            key_part = nn(grads, query_block)
            if step:
                value_part += value_acc[low:high]
                key_part += key_acc[low:high]
            value_acc[low:high] = value_part
            key_acc[low:high] = key_part

    coarse_out = (coarse_key_grad, coarse_value_grad)
    for slot, acc in enumerate((key_acc, value_acc)):
        part = acc[span:].astype(jnp.bfloat16)
        if not direct:
            hand_out(4 + slot, part, coarse_out[slot])
            continue
        coarse_stage[slot] = part
        for step_core in range(CORES):
            for step_sub in range(n_sub):
                for step_dp in range(n_dp):
                    to_core = lax.rem(core + step_core, CORES)
                    to_sub = lax.rem(sub + step_sub, n_sub)
                    to_dp = lax.rem(dp + step_dp, n_dp)
                    piece = (to_core * n_sub + to_sub) * n_dp + to_dp
                    src = coarse_stage.at[slot, pl.ds(pl.multiple_of(piece * mine, mine), mine)]
                    dst = coarse_out[slot].at[dp, :, head_columns(sub * CORES + core)]
                    if step_core or step_sub or step_dp:
                        remote(
                            src,
                            dst,
                            cg_send.at[slot],
                            cg_recv.at[slot],
                            (chip * CORES + to_core, to_sub, to_dp),
                        )
                    else:
                        pltpu.make_async_copy(src, dst, cg_recv.at[slot]).start()
    hand_out(2, key_acc[:span].astype(jnp.bfloat16), key_grad)
    hand_out(3, value_acc[:span].astype(jnp.bfloat16), value_grad)

    collect(0, attended)
    collect(1, query_grad)
    collect(2, key_grad)
    collect(3, value_grad)
    for slot in range(2):
        if direct:
            wait_bytes(coarse_out[slot], cg_recv.at[slot])
            wait_bytes(coarse_stage.at[slot, : coarse_span - mine], cg_send.at[slot])
        else:
            collect(4 + slot, coarse_out[slot])
    for index, (buffer, size, send) in enumerate(
        ((kv, span, kv_send), (ckv, coarse_span, c_send), (qg, span, qg_send))
    ):
        for hop in range(chips - 1):
            for right in (0, 1):
                at = chip - hop if right else chip + hop
                had = jnp.logical_and(at >= 0, chip + 1 < chips) if right else jnp.logical_and(
                    at < chips, chip >= 1
                )
                block = buffer.at[:, block_of(chip, size)]
                pl.when(had)(
                    lambda block=block, sem=send.at[right, hop]: wait_bytes(block, sem)
                )
    wait_bytes(kv.at[:, my_rows], near_send.at[0])
    wait_bytes(qg.at[:, my_rows], near_send.at[1])
    wait_bytes(ckv.at[:, : coarse_span - mine], near_send.at[2])
    wait_bytes(stats.at[: chips - 1], stat_send)


def fused(sizes, direct, queries, keys, values, out_grad, coarse_keys, coarse_values, fine_scale):
    n_fine, n_sub, n_dp = sizes
    rows, width = queries.shape[1:]
    total = rows * n_fine
    chips, span = n_fine // CORES, rows * CORES
    coarse_total = coarse_keys.shape[1] * n_fine * (n_sub * n_dp if direct else 1)
    coarse_span = coarse_total // chips
    bf16, f32 = jnp.bfloat16, jnp.float32
    hbm_spec = pl.BlockSpec(memory_space=pltpu.HBM)
    vmem_spec = pl.BlockSpec(memory_space=pltpu.VMEM)
    dma = pltpu.SemaphoreType.DMA
    return pl.pallas_call(
        functools.partial(kernel, sizes, direct),
        out_shape=[jax.ShapeDtypeStruct(queries.shape, bf16)] * 4
        + [jax.ShapeDtypeStruct(coarse_keys.shape, bf16)] * 2,
        in_specs=[hbm_spec] * 7,
        out_specs=[vmem_spec] * 6,
        scratch_shapes=[
            pltpu.VMEM((1, fine_scale.shape[0]), jnp.int32),
            pltpu.VMEM((2, rows, width), bf16),
            pltpu.VMEM((2, rows, width), bf16),
            pltpu.VMEM((2,) + coarse_keys.shape, bf16),
            pltpu.VMEM((2, total, HEAD), bf16),
            pltpu.VMEM((2, total, HEAD), bf16),
            pltpu.VMEM((2, coarse_total, HEAD), bf16),
            pltpu.VMEM((chips, 8, span), f32),
            pltpu.VMEM((6, span, HEAD), bf16),
            pltpu.VMEM((2, coarse_span, HEAD), bf16),
            pltpu.VMEM((span + coarse_span, HEAD), f32),
            pltpu.VMEM((span + coarse_span, HEAD), f32),
            dma((7,)),
            dma((chips,)),
            dma((chips,)),
            dma((chips,)),
            dma((chips,)),
            dma((6,)),
            dma((2,)),
            dma((2, chips)),
            dma((2, chips)),
            dma((2, chips)),
            dma((3,)),
            dma,
            dma((6,)),
            dma((2,)),
        ],
        compiler_params=pltpu.CompilerParams(
            collective_id=0, has_side_effects=True, vmem_limit_bytes=48 * 1024 * 1024
        ),
    )(
        *(
            pltpu.with_memory_space_constraint(argument, pltpu.HBM)
            for argument in (
                queries,
                keys,
                values,
                out_grad,
                coarse_keys,
                coarse_values,
                fine_scale.reshape(1, fine_scale.shape[0]),
            )
        )
    )


def place(count, *refs):
    sem = refs[2 * count]
    stores = [
        pltpu.make_async_copy(refs[i], refs[count + i], sem.at[i]) for i in range(count)
    ]
    for store in stores:
        store.start()
    for store in stores:
        store.wait()


def placed_out(results):
    count = len(results)
    return pl.pallas_call(
        functools.partial(place, count),
        out_shape=[jax.ShapeDtypeStruct(result.shape, result.dtype) for result in results],
        in_specs=[pl.BlockSpec(memory_space=pltpu.VMEM)] * count,
        out_specs=[pl.BlockSpec(memory_space=pltpu.HBM)] * count,
        scratch_shapes=[pltpu.SemaphoreType.DMA((count,))],
        compiler_params=pltpu.CompilerParams(vmem_limit_bytes=8 * 1024 * 1024),
    )(*results)


def shards(sizes, queries, keys, values, out_grad, coarse_keys, coarse_values, fine_scale):
    direct = coarse_keys.shape[1] % 16 == 0
    fine = (queries, keys, values, out_grad)
    if direct:
        return tuple(placed_out(fused(sizes, True, *fine, coarse_keys, coarse_values, fine_scale)))

    def gathered(coarse):
        image = lax.all_to_all(coarse, "dp", split_axis=0, concat_axis=1, tiled=True)
        return lax.all_to_all(image, "sub", split_axis=2, concat_axis=1, tiled=True)

    def returned(grad):
        back = lax.all_to_all(grad, "sub", split_axis=1, concat_axis=2, tiled=True)
        return lax.all_to_all(back, "dp", split_axis=1, concat_axis=0, tiled=True)

    results = fused(sizes, False, *fine, gathered(coarse_keys), gathered(coarse_values), fine_scale)
    return tuple(results[:4]) + (returned(results[4]), returned(results[5]))


def solution(mesh):
    sizes = tuple(mesh.shape[name] for name in ("fine", "sub", "dp"))
    placed = P("dp", "fine", "sub")
    coarse = P(None, ("fine", "sub", "dp"), None)
    return jax.shard_map(
        functools.partial(shards, sizes),
        mesh=mesh,
        in_specs=(placed,) * 4 + (coarse, coarse, P()),
        out_specs=(placed,) * 4 + (coarse, coarse),
        check_vma=False,
    )
```

profile of v0, /device:TPU:0, one launch (start us, length us, event | category | flops | bytes accessed | tf_op | source)
XLA Modules:
  0.0 36.6 jit_solution(6418887424439341169)
XLA Ops:
  0.6 35.2 %shard_map.118 = (bf16[1,128,256]{2,1,0:T(8,128)(2,1)S(1)}, bf16[1,128,256]{2,1,0:T(8,128)(2,1)S(1)}, bf16[1,128,256]{2,1,0:T(8,128)(2,1)S(1)}, bf16[1,128,256]{...) custom-call(bf16[1,128,256]{2,1,0:T(8,128)(2,1)} %queries.1, ...), custom_call_target="tpu_custom_call" | custom-call | tf_op jit(solution)/shard_map/pallas_call | solution.py:407
  35.8 0.8 %shard_map.119 = (bf16[1,128,256]{2,1,0:T(8,128)(2,1)}, bf16[1,128,256]{2,1,0:T(8,128)(2,1)}, bf16[1,128,256]{2,1,0:T(8,128)(2,1)}, bf16[1,128,256]{2,1,0:T(8,12...) custom-call(bf16[1,128,256]{2,1,0:T(8,128)(2,1)S(1)} %get-tuple-element.12.refs_0_, ...), custom_call_target="tpu_custom_call" | custom-call | tf_op jit(solution)/shard_map/pallas_call | solution.py:473
where the time goes:
time: 36.7 us; the launch traced here: 36.6 us
  Pallas kernels  35.9 us (98%)
  between operations  0.64 us (2%)
    pallas_call x1, Pallas kernels, fused(): pl.pallas_call(functools.partial(kernel, sizes, direct), out_shape=[jax.S...  35.2 us
    pallas_call x1, Pallas kernels, placed_out(): pl.pallas_call(functools.partial(place, count), out_shape=[jax.ShapeDtype...  0.77 us

commit v1 on v0

--- a/solution.py
+++ b/solution.py
@@ -16,6 +16,10 @@
 
 def nt(a, b):
     return lax.dot_general(a, b, (((1,), (1,)), ((), ())), preferred_element_type=jnp.float32)
+
+
+def tn(a, b):
+    return lax.dot_general(a, b, (((0,), (0,)), ((), ())), preferred_element_type=jnp.float32)
 
 
 def nn(a, b):
@@ -393,7 +397,7 @@
     wait_bytes(stats.at[: chips - 1], stat_send)
 
 
-def fused(sizes, direct, queries, keys, values, out_grad, coarse_keys, coarse_values, fine_scale):
+def fused(sizes, queries, keys, values, out_grad, coarse_keys, coarse_values, fine_scale, direct):
     n_fine, n_sub, n_dp = sizes
     rows, width = queries.shape[1:]
     total = rows * n_fine
@@ -457,6 +461,440 @@
     )
 
 
+def host_kernel(
+    sizes,
+    queries,
+    keys,
+    values,
+    out_grad,
+    coarse_keys,
+    coarse_values,
+    scale_in,
+    attended,
+    query_grad,
+    key_grad,
+    value_grad,
+    coarse_key_grad,
+    coarse_value_grad,
+    scale_row,
+    kv_src,
+    qg_src,
+    c_src,
+    plane_in,
+    kv,
+    qg,
+    stage,
+    key_acc,
+    value_acc,
+    swap_out,
+    swap_in,
+    total_out,
+    load_sem,
+    own_sem,
+    plane_recv,
+    kv_recv,
+    c_recv,
+    qg_recv,
+    near_recv,
+    swap_recv,
+    out_recv,
+    coarse_recv,
+    plane_send,
+    kv_send,
+    c_send,
+    qg_send,
+    near_send,
+    swap_send,
+    row_send,
+    key_send,
+    coarse_send,
+):
+    n_fine, n_sub, n_dp = sizes
+    fine, sub, dp = lax.axis_index("fine"), lax.axis_index("sub"), lax.axis_index("dp")
+    chip, core = fine // CORES, lax.rem(fine, CORES)
+    chips = n_fine // CORES
+    first_host = chips // 2 - 1
+    heads = queries.shape[2] // HEAD
+    rows = keys.shape[1]
+    mine = coarse_keys.shape[1]
+    crows = mine * n_sub * n_dp
+    half, chalf = chips * rows, chips * crows
+    fines = CORES * half
+    partner = {"fine": chip * CORES + (1 - core)}
+    unit = chip - first_host
+    hosting = jnp.logical_and(unit >= 0, unit < heads)
+    left = chip < chips // 2
+
+    def head_columns(index, count=1):
+        return pl.ds(pl.multiple_of(index * HEAD, HEAD), count * HEAD)
+
+    def block_of(at, size):
+        return pl.ds(pl.multiple_of(at * size, size), size)
+
+    def fine_rows(owner, at):
+        return block_of(owner * chips + at, rows)
+
+    def coarse_rows(owner, at):
+        return pl.ds(pl.multiple_of(fines + (owner * chips + at) * crows, crows), crows)
+
+    def load(src, dst, sem):
+        copy = pltpu.make_async_copy(src, dst, sem)
+        copy.start()
+        return copy
+
+    def remote(src, dst, send, recv, device):
+        pltpu.make_async_remote_copy(
+            src_ref=src,
+            dst_ref=dst,
+            send_sem=send,
+            recv_sem=recv,
+            device_id=device,
+            device_id_type=MESH,
+        ).start()
+
+    my_slot = sub * n_dp + dp
+    loads = [
+        load(src, dst, load_sem.at[slot])
+        for slot, (src, dst) in enumerate(
+            (
+                (coarse_keys, c_src.at[0]),
+                (coarse_values, c_src.at[1]),
+                (keys.at[0], kv_src.at[0]),
+                (values.at[0], kv_src.at[1]),
+                (queries.at[0], qg_src.at[0]),
+                (out_grad.at[0], qg_src.at[1]),
+                (scale_in, scale_row),
+                (
+                    coarse_keys.at[dp, :, head_columns(sub * heads, heads)],
+                    plane_in.at[0, block_of(my_slot, mine)],
+                ),
+                (
+                    coarse_values.at[dp, :, head_columns(sub * heads, heads)],
+                    plane_in.at[1, block_of(my_slot, mine)],
+                ),
+            )
+        )
+    ]
+    own_pairs = (
+        (keys, kv.at[0, fine_rows(core, chip)]),
+        (values, kv.at[1, fine_rows(core, chip)]),
+        (queries, qg.at[0, block_of(chip, rows)]),
+        (out_grad, qg.at[1, block_of(chip, rows)]),
+    )
+
+    @pl.when(hosting)
+    def _():
+        for slot, (src, dst) in enumerate(own_pairs):
+            load(src.at[0, :, head_columns(unit)], dst, own_sem.at[slot])
+
+    barrier = pltpu.get_barrier_semaphore()
+
+    def greet(device):
+        pl.semaphore_signal(barrier, inc=1, device_id=device, device_id_type=MESH)
+
+    plane = []
+    for step_sub in range(n_sub):
+        for step_dp in range(n_dp):
+            if step_sub or step_dp:
+                plane.append((lax.rem(sub + step_sub, n_sub), lax.rem(dp + step_dp, n_dp)))
+    for to_sub, to_dp in plane:
+        greet((fine, to_sub, to_dp))
+    pl.when(hosting)(lambda: greet((partner["fine"], sub, dp)))
+    for step in range(1, chips):
+        to = lax.rem(chip + step, chips)
+        to_host = jnp.logical_and(to >= first_host, to < first_host + heads)
+        pl.when(jnp.logical_or(hosting, to_host))(
+            lambda to=to: greet((to * CORES + core, sub, dp))
+        )
+    pl.semaphore_wait(barrier, len(plane) + jnp.where(hosting, chips, heads))
+
+    for at in (0, 1):
+        loads[at].wait()
+    for index, (to_sub, to_dp) in enumerate(plane):
+        remote(
+            c_src.at[:, to_dp, :, head_columns(to_sub * heads, heads)],
+            plane_in.at[:, block_of(my_slot, mine)],
+            plane_send.at[index],
+            plane_recv,
+            (fine, to_sub, to_dp),
+        )
+
+    def to_hosts(far_first, src, dst, send, recv):
+        for step in range(heads):
+            nth = jnp.where(left, step, heads - 1 - step)
+            head = heads - 1 - nth if far_first else nth
+            host = first_host + head
+            pl.when(host != chip)(
+                lambda head=head, host=host: remote(
+                    src.at[:, :, head_columns(head)],
+                    dst,
+                    send.at[head],
+                    recv.at[chip],
+                    {"fine": host * CORES + core},
+                )
+            )
+
+    for at in (2, 3):
+        loads[at].wait()
+    to_hosts(True, kv_src, kv.at[:, fine_rows(core, chip)], kv_send, kv_recv)
+    for at in (7, 8):
+        loads[at].wait()
+    wait_bytes(plane_in.at[:, : crows - mine], plane_recv)
+    to_hosts(True, plane_in, kv.at[:, coarse_rows(core, chip)], c_send, c_recv)
+    for at in (4, 5):
+        loads[at].wait()
+    to_hosts(False, qg_src, qg.at[:, block_of(chip, rows)], qg_send, qg_recv)
+    loads[6].wait()
+
+    outs = (attended, query_grad, key_grad, value_grad)
+    coarse_outs = (coarse_key_grad, coarse_value_grad)
+
+    @pl.when(hosting)
+    def _():
+        columns = head_columns(unit)
+        away = jnp.where(unit == 0, 1, -1)
+        offsets = [0]
+        for reach in range(1, chips // 2 + 1):
+            offsets += [reach, -reach]
+        offsets = offsets[:chips]
+        order = [chip + away * offset for offset in offsets]
+
+        def pass_near(block, index):
+            remote(block, block, near_send.at[index], near_recv.at[index], partner)
+
+        for index, (src, dst) in enumerate(own_pairs):
+            pltpu.make_async_copy(src.at[0, :, columns], dst, own_sem.at[index]).wait()
+        pass_near(kv.at[:, fine_rows(core, chip)], 0)
+        own_coarse = plane_in.at[:, :, columns]
+        remote(
+            own_coarse,
+            kv.at[:, coarse_rows(core, chip)],
+            near_send.at[chips],
+            near_recv.at[chips],
+            partner,
+        )
+        kv[:, coarse_rows(core, chip)] = own_coarse[...]
+        for index, at in list(enumerate(order))[1:]:
+            block = kv.at[:, fine_rows(core, at)]
+            wait_bytes(block, kv_recv.at[at])
+            pass_near(block, index)
+        for index, at in list(enumerate(order))[1:]:
+            block = kv.at[:, coarse_rows(core, at)]
+            wait_bytes(block, c_recv.at[at])
+            pass_near(block, chips + index)
+
+        key_scale = jnp.concatenate(
+            [
+                scale_row[:, (at * CORES + owner) * rows : (at * CORES + owner + 1) * rows]
+                for owner in range(CORES)
+                for at in range(chips)
+            ],
+            axis=1,
+        )
+        for index, at in enumerate(order):
+            wait_bytes(kv.at[:, fine_rows(1 - core, at)], near_recv.at[index])
+        for index, at in enumerate(order):
+            wait_bytes(kv.at[:, coarse_rows(1 - core, at)], near_recv.at[chips + index])
+
+        for index, at in enumerate(order):
+            block_rows = block_of(at, rows)
+            if index:
+                wait_bytes(qg.at[:, block_rows], qg_recv.at[at])
+            query, grad = qg[0, block_rows], qg[1, block_rows]
+            own_scale = scale_row[:, block_of(at * CORES + core, rows)]
+            own_column = jnp.transpose(jnp.broadcast_to(own_scale, (HEAD, rows)))[:, :1]
+            scores = nt(query, kv[0])
+            scores = jnp.concatenate(
+                [
+                    jnp.where(key_scale <= own_column, scores[:, :fines], -jnp.inf),
+                    scores[:, fines:],
+                ],
+                axis=1,
+            )
+            peak = jnp.max(scores, axis=1, keepdims=True)
+            powers = jnp.exp((scores - peak) * INVERSE)
+            scale = 1.0 / jnp.sum(powers, axis=1, keepdims=True)
+            weights = powers * scale
+            dots = nt(grad, kv[1])
+            delta = jnp.sum(weights * dots, axis=1, keepdims=True)
+            weights = weights.astype(jnp.bfloat16)
+            grads = (weights.astype(jnp.float32) * (dots - delta) * INVERSE).astype(jnp.bfloat16)
+            out = nn(weights, kv[1]).astype(jnp.bfloat16)
+            query_out = nn(grads, kv[0]).astype(jnp.bfloat16)
+            for slot, value in enumerate((out, query_out)):
+                if not index:
+                    outs[slot][0, :, columns] = value
+                    continue
+                stage[slot, index - 1] = value
+                remote(
+                    stage.at[slot, index - 1],
+                    outs[slot].at[0, :, columns],
+                    row_send.at[slot, index - 1],
+                    out_recv.at[slot, unit],
+                    {"fine": at * CORES + core},
+                )
+            value_part, key_part = tn(weights, grad), tn(grads, query)
+            if index:
+                value_part += value_acc[...]
+                key_part += key_acc[...]
+            value_acc[...] = value_part
+            key_acc[...] = key_part
+
+        accs = (key_acc, value_acc)
+        for slot in (1, 0):
+            swap_out[slot, :half] = accs[slot][block_of(1 - core, half)].astype(jnp.bfloat16)
+            swap_out[slot, half:] = accs[slot][
+                pl.ds(pl.multiple_of(fines + (1 - core) * chalf, chalf), chalf)
+            ].astype(jnp.bfloat16)
+            remote(
+                swap_out.at[slot], swap_in.at[slot], swap_send.at[slot], swap_recv.at[slot], partner
+            )
+        for slot in (1, 0):
+            wait_bytes(swap_in.at[slot], swap_recv.at[slot])
+            total_out[slot, :half] = (
+                accs[slot][block_of(core, half)] + swap_in[slot, :half].astype(jnp.float32)
+            ).astype(jnp.bfloat16)
+            total_out[slot, half:] = (
+                accs[slot][pl.ds(pl.multiple_of(fines + core * chalf, chalf), chalf)]
+                + swap_in[slot, half:].astype(jnp.float32)
+            ).astype(jnp.bfloat16)
+            result = outs[2 + slot]
+            for index, at in reversed(list(enumerate(order))):
+                block = total_out.at[slot, block_of(at, rows)]
+                if index:
+                    remote(
+                        block,
+                        result.at[0, :, columns],
+                        key_send.at[slot, index - 1],
+                        out_recv.at[2 + slot, unit],
+                        {"fine": at * CORES + core},
+                    )
+                else:
+                    result[0, :, columns] = block[...]
+                for to_sub, to_dp in [(sub, dp)] + plane:
+                    piece = (at * n_sub + to_sub) * n_dp + to_dp
+                    src = total_out.at[
+                        slot, pl.ds(pl.multiple_of(half + piece * mine, mine), mine)
+                    ]
+                    dst = coarse_outs[slot].at[dp, :, head_columns(sub * heads + unit)]
+                    if index == 0 and to_sub is sub and to_dp is dp:
+                        pltpu.make_async_copy(src, dst, coarse_recv.at[slot]).start()
+                    else:
+                        remote(
+                            src,
+                            dst,
+                            coarse_send.at[slot],
+                            coarse_recv.at[slot],
+                            (at * CORES + core, to_sub, to_dp),
+                        )
+
+    for head in range(heads):
+
+        @pl.when(first_host + head != chip)
+        def _(head=head):
+            for slot, result in enumerate(outs):
+                wait_bytes(
+                    result.at[0, :, head * HEAD : (head + 1) * HEAD], out_recv.at[slot, head]
+                )
+
+    for slot, result in enumerate(coarse_outs):
+        wait_bytes(result, coarse_recv.at[slot])
+    for index in range(len(plane)):
+        wait_bytes(c_src.at[:, 0, :, : heads * HEAD], plane_send.at[index])
+    for head in range(heads):
+
+        @pl.when(first_host + head != chip)
+        def _(head=head):
+            wait_bytes(kv_src.at[:, :, :HEAD], kv_send.at[head])
+            wait_bytes(plane_in.at[:, :, :HEAD], c_send.at[head])
+            wait_bytes(qg_src.at[:, :, :HEAD], qg_send.at[head])
+
+    @pl.when(hosting)
+    def _():
+        for index in range(chips):
+            wait_bytes(kv.at[:, :rows], near_send.at[index])
+            wait_bytes(kv.at[:, fines : fines + crows], near_send.at[chips + index])
+        for slot in range(2):
+            wait_bytes(swap_out.at[slot], swap_send.at[slot])
+            for index in range(chips - 1):
+                wait_bytes(stage.at[slot, index], row_send.at[slot, index])
+                wait_bytes(total_out.at[slot, :rows], key_send.at[slot, index])
+            wait_bytes(total_out.at[slot, : chalf - mine], coarse_send.at[slot])
+
+
+def fits_hosts(sizes, queries):
+    chips, heads = sizes[0] // CORES, queries.shape[2] // HEAD
+    return heads == CORES and chips % 2 == 0 and chips <= 2 * CORES
+
+
+def hosted(sizes, queries, keys, values, out_grad, coarse_keys, coarse_values, fine_scale):
+    n_fine, n_sub, n_dp = sizes
+    rows, width = queries.shape[1:]
+    heads, chips, mine = width // HEAD, n_fine // CORES, coarse_keys.shape[1]
+    crows = mine * n_sub * n_dp
+    half = chips * (rows + crows)
+    total = CORES * half
+    bf16, f32 = jnp.bfloat16, jnp.float32
+    dma = pltpu.SemaphoreType.DMA
+    return pl.pallas_call(
+        functools.partial(host_kernel, sizes),
+        out_shape=[jax.ShapeDtypeStruct(queries.shape, bf16)] * 4
+        + [jax.ShapeDtypeStruct(coarse_keys.shape, bf16)] * 2,
+        in_specs=[pl.BlockSpec(memory_space=pltpu.HBM)] * 7,
+        out_specs=[pl.BlockSpec(memory_space=pltpu.VMEM)] * 6,
+        scratch_shapes=[
+            pltpu.VMEM((1, fine_scale.shape[0]), jnp.int32),
+            pltpu.VMEM((2, rows, width), bf16),
+            pltpu.VMEM((2, rows, width), bf16),
+            pltpu.VMEM((2,) + coarse_keys.shape, bf16),
+            pltpu.VMEM((2, crows, width), bf16),
+            pltpu.VMEM((2, total, HEAD), bf16),
+            pltpu.VMEM((2, chips * rows, HEAD), bf16),
+            pltpu.VMEM((2, chips - 1, rows, HEAD), bf16),
+            pltpu.VMEM((total, HEAD), f32),
+            pltpu.VMEM((total, HEAD), f32),
+            pltpu.VMEM((2, half, HEAD), bf16),
+            pltpu.VMEM((2, half, HEAD), bf16),
+            pltpu.VMEM((2, half, HEAD), bf16),
+            dma((9,)),
+            dma((4,)),
+            dma,
+            dma((chips,)),
+            dma((chips,)),
+            dma((chips,)),
+            dma((2 * chips,)),
+            dma((2,)),
+            dma((4, heads)),
+            dma((2,)),
+            dma((n_sub * n_dp - 1,)),
+            dma((heads,)),
+            dma((heads,)),
+            dma((heads,)),
+            dma((2 * chips,)),
+            dma((2,)),
+            dma((2, chips - 1)),
+            dma((2, chips - 1)),
+            dma((2,)),
+        ],
+        compiler_params=pltpu.CompilerParams(
+            collective_id=0, has_side_effects=True, vmem_limit_bytes=48 * 1024 * 1024
+        ),
+    )(
+        *(
+            pltpu.with_memory_space_constraint(argument, pltpu.HBM)
+            for argument in (
+                queries,
+                keys,
+                values,
+                out_grad,
+                coarse_keys,
+                coarse_values,
+                fine_scale.reshape(1, fine_scale.shape[0]),
+            )
+        )
+    )
+
+
 def place(count, *refs):
     sem = refs[2 * count]
     stores = [
@@ -484,7 +922,8 @@
     direct = coarse_keys.shape[1] % 16 == 0
     fine = (queries, keys, values, out_grad)
     if direct:
-        return tuple(placed_out(fused(sizes, True, *fine, coarse_keys, coarse_values, fine_scale)))
+        call = hosted if fits_hosts(sizes, queries) else functools.partial(fused, direct=True)
+        return tuple(placed_out(call(sizes, *fine, coarse_keys, coarse_values, fine_scale)))
 
     def gathered(coarse):
         image = lax.all_to_all(coarse, "dp", split_axis=0, concat_axis=1, tiled=True)
@@ -494,7 +933,9 @@
         back = lax.all_to_all(grad, "sub", split_axis=1, concat_axis=2, tiled=True)
         return lax.all_to_all(back, "dp", split_axis=1, concat_axis=0, tiled=True)
 
-    results = fused(sizes, False, *fine, gathered(coarse_keys), gathered(coarse_values), fine_scale)
+    results = fused(
+        sizes, *fine, gathered(coarse_keys), gathered(coarse_values), fine_scale, direct=False
+    )
     return tuple(results[:4]) + (returned(results[4]), returned(results[5]))
 
 

time: 36.7 us -> 28.4 us (0.77)
  Pallas kernels: 35.9 us -> 27.6 us
    pallas_call x1, Pallas kernels: 35.2 us -> 26.9 us  [hosted(): pl.pallas_call(functools.partial(host_kernel, sizes), out_shape=[jax.Shap...]
where the time goes in v1:
time: 28.4 us; the launch traced here: 28.3 us
  Pallas kernels  27.6 us (97%)
  between operations  0.64 us (2%)
    pallas_call x1, Pallas kernels, hosted(): pl.pallas_call(functools.partial(host_kernel, sizes), out_shape=[jax.Shap...  26.9 us
    pallas_call x1, Pallas kernels, placed_out(): pl.pallas_call(functools.partial(place, count), out_shape=[jax.ShapeDtype...  0.77 us

profile of v1, /device:TPU:0, one launch (start us, length us, event | category | flops | bytes accessed | tf_op | source)
XLA Modules:
  0.0 28.3 jit_solution(14656240590744341741)
XLA Ops:
  0.6 26.9 %shard_map.118 = (bf16[1,128,256]{2,1,0:T(8,128)(2,1)S(1)}, bf16[1,128,256]{2,1,0:T(8,128)(2,1)S(1)}, bf16[1,128,256]{2,1,0:T(8,128)(2,1)S(1)}, bf16[1,128,256]{...) custom-call(bf16[1,128,256]{2,1,0:T(8,128)(2,1)} %queries.1, ...), custom_call_target="tpu_custom_call" | custom-call | tf_op jit(solution)/shard_map/pallas_call | solution.py:839
  27.5 0.8 %shard_map.119 = (bf16[1,128,256]{2,1,0:T(8,128)(2,1)}, bf16[1,128,256]{2,1,0:T(8,128)(2,1)}, bf16[1,128,256]{2,1,0:T(8,128)(2,1)}, bf16[1,128,256]{2,1,0:T(8,12...) custom-call(bf16[1,128,256]{2,1,0:T(8,128)(2,1)S(1)} %get-tuple-element.12.refs_0_, ...), custom_call_target="tpu_custom_call" | custom-call | tf_op jit(solution)/shard_map/pallas_call | solution.py:911

commit v2 on v1

--- a/solution.py
+++ b/solution.py
@@ -12,6 +12,7 @@
 CORES = 2
 MESH = pl.DeviceIdType.MESH
 INVERSE = 1.0 / math.sqrt(HEAD)
+LOG2E = math.log2(math.e)
 
 
 def nt(a, b):
@@ -482,6 +483,7 @@
     c_src,
     plane_in,
     kv,
+    flipped,
     qg,
     stage,
     key_acc,
@@ -518,8 +520,8 @@
     rows = keys.shape[1]
     mine = coarse_keys.shape[1]
     crows = mine * n_sub * n_dp
-    half, chalf = chips * rows, chips * crows
-    fines = CORES * half
+    half = chips * rows
+    share = half + chips * crows
     partner = {"fine": chip * CORES + (1 - core)}
     unit = chip - first_host
     hosting = jnp.logical_and(unit >= 0, unit < heads)
@@ -531,11 +533,11 @@
     def block_of(at, size):
         return pl.ds(pl.multiple_of(at * size, size), size)
 
-    def fine_rows(owner, at):
-        return block_of(owner * chips + at, rows)
-
-    def coarse_rows(owner, at):
-        return pl.ds(pl.multiple_of(fines + (owner * chips + at) * crows, crows), crows)
+    def fine_rows(part, at):
+        return pl.ds(pl.multiple_of(part * share + at * rows, rows), rows)
+
+    def coarse_rows(part, at):
+        return pl.ds(pl.multiple_of(part * share + half + at * crows, crows), crows)
 
     def load(src, dst, sem):
         copy = pltpu.make_async_copy(src, dst, sem)
@@ -576,8 +578,8 @@
         )
     ]
     own_pairs = (
-        (keys, kv.at[0, fine_rows(core, chip)]),
-        (values, kv.at[1, fine_rows(core, chip)]),
+        (keys, kv.at[0, fine_rows(0, chip)]),
+        (values, kv.at[1, fine_rows(0, chip)]),
         (queries, qg.at[0, block_of(chip, rows)]),
         (out_grad, qg.at[1, block_of(chip, rows)]),
     )
@@ -602,11 +604,8 @@
     pl.when(hosting)(lambda: greet((partner["fine"], sub, dp)))
     for step in range(1, chips):
         to = lax.rem(chip + step, chips)
-        to_host = jnp.logical_and(to >= first_host, to < first_host + heads)
-        pl.when(jnp.logical_or(hosting, to_host))(
-            lambda to=to: greet((to * CORES + core, sub, dp))
-        )
-    pl.semaphore_wait(barrier, len(plane) + jnp.where(hosting, chips, heads))
+        pl.when(hosting)(lambda to=to: greet((to * CORES + core, sub, dp)))
+    pl.semaphore_wait(barrier, len(plane) + heads)
 
     for at in (0, 1):
         loads[at].wait()
@@ -619,174 +618,204 @@
             (fine, to_sub, to_dp),
         )
 
-    def to_hosts(far_first, src, dst, send, recv):
-        for step in range(heads):
-            nth = jnp.where(left, step, heads - 1 - step)
-            head = heads - 1 - nth if far_first else nth
-            host = first_host + head
-            pl.when(host != chip)(
-                lambda head=head, host=host: remote(
-                    src.at[:, :, head_columns(head)],
-                    dst,
-                    send.at[head],
-                    recv.at[chip],
-                    {"fine": host * CORES + core},
-                )
+    def to_host(nth, src, dst, send, recv):
+        head = jnp.where(left, nth, heads - 1 - nth)
+        host = first_host + head
+        pl.when(host != chip)(
+            lambda: remote(
+                src.at[:, :, head_columns(head)],
+                dst,
+                send.at[head],
+                recv.at[chip],
+                {"fine": host * CORES + core},
             )
-
+        )
+
+    def give_queries(nth):
+        to_host(nth, qg_src, qg.at[:, block_of(chip, rows)], qg_send, qg_recv)
+
+    near_to_far = range(heads)
     for at in (2, 3):
         loads[at].wait()
-    to_hosts(True, kv_src, kv.at[:, fine_rows(core, chip)], kv_send, kv_recv)
+    for nth in reversed(near_to_far):
+        to_host(nth, kv_src, kv.at[:, fine_rows(0, chip)], kv_send, kv_recv)
+    for at in (4, 5):
+        loads[at].wait()
+    pl.when(left)(lambda: give_queries(heads - 1))
     for at in (7, 8):
         loads[at].wait()
     wait_bytes(plane_in.at[:, : crows - mine], plane_recv)
-    to_hosts(True, plane_in, kv.at[:, coarse_rows(core, chip)], c_send, c_recv)
-    for at in (4, 5):
-        loads[at].wait()
-    to_hosts(False, qg_src, qg.at[:, block_of(chip, rows)], qg_send, qg_recv)
+    for nth in reversed(near_to_far):
+        to_host(nth, plane_in, kv.at[:, coarse_rows(0, chip)], c_send, c_recv)
+    for nth in near_to_far[:-1]:
+        give_queries(nth)
+    pl.when(jnp.logical_not(left))(lambda: give_queries(heads - 1))
     loads[6].wait()
 
     outs = (attended, query_grad, key_grad, value_grad)
     coarse_outs = (coarse_key_grad, coarse_value_grad)
+    accs = (key_acc, value_acc)
 
     @pl.when(hosting)
     def _():
         columns = head_columns(unit)
-        away = jnp.where(unit == 0, 1, -1)
-        offsets = [0]
-        for reach in range(1, chips // 2 + 1):
-            offsets += [reach, -reach]
-        offsets = offsets[:chips]
-        order = [chip + away * offset for offset in offsets]
-
-        def pass_near(block, index):
-            remote(block, block, near_send.at[index], near_recv.at[index], partner)
+        other_host = 2 * first_host + 1 - chip
+        others, given = [other_host], [other_host]
+        if chips > CORES:
+            first, last_end = 0 * chip, 0 * chip + chips - 1
+            pick = functools.partial(jnp.where, unit == 0)
+            others = [pick(other_host, first), pick(first, other_host), last_end]
+            given = [first, last_end, other_host]
+        order = [chip] + others
+
+        def pass_near(block, dst, index):
+            remote(block, dst, near_send.at[index], near_recv.at[index], partner)
 
         for index, (src, dst) in enumerate(own_pairs):
             pltpu.make_async_copy(src.at[0, :, columns], dst, own_sem.at[index]).wait()
-        pass_near(kv.at[:, fine_rows(core, chip)], 0)
         own_coarse = plane_in.at[:, :, columns]
-        remote(
-            own_coarse,
-            kv.at[:, coarse_rows(core, chip)],
-            near_send.at[chips],
-            near_recv.at[chips],
-            partner,
-        )
-        kv[:, coarse_rows(core, chip)] = own_coarse[...]
-        for index, at in list(enumerate(order))[1:]:
-            block = kv.at[:, fine_rows(core, at)]
+        pass_near(kv.at[:, fine_rows(0, chip)], kv.at[:, fine_rows(1, chip)], 0)
+        pass_near(own_coarse, kv.at[:, coarse_rows(1, chip)], chips)
+        kv[:, coarse_rows(0, chip)] = own_coarse[...]
+        for index, at in enumerate(others):
+            block = kv.at[:, fine_rows(0, at)]
             wait_bytes(block, kv_recv.at[at])
-            pass_near(block, index)
-        for index, at in list(enumerate(order))[1:]:
-            block = kv.at[:, coarse_rows(core, at)]
+            pass_near(block, kv.at[:, fine_rows(1, at)], 1 + index)
+
+        def flip(low, high):
+            for slot in range(2):
+                flipped[slot, :, low:high] = jnp.transpose(kv[slot, low:high])
+
+        flip(0, half)
+        for index, at in enumerate(others):
+            block = kv.at[:, coarse_rows(0, at)]
             wait_bytes(block, c_recv.at[at])
-            pass_near(block, chips + index)
-
-        key_scale = jnp.concatenate(
-            [
-                scale_row[:, (at * CORES + owner) * rows : (at * CORES + owner + 1) * rows]
-                for owner in range(CORES)
-                for at in range(chips)
-            ],
-            axis=1,
-        )
-        for index, at in enumerate(order):
-            wait_bytes(kv.at[:, fine_rows(1 - core, at)], near_recv.at[index])
-        for index, at in enumerate(order):
-            wait_bytes(kv.at[:, coarse_rows(1 - core, at)], near_recv.at[chips + index])
-
-        for index, at in enumerate(order):
-            block_rows = block_of(at, rows)
-            if index:
-                wait_bytes(qg.at[:, block_rows], qg_recv.at[at])
-            query, grad = qg[0, block_rows], qg[1, block_rows]
-            own_scale = scale_row[:, block_of(at * CORES + core, rows)]
-            own_column = jnp.transpose(jnp.broadcast_to(own_scale, (HEAD, rows)))[:, :1]
-            scores = nt(query, kv[0])
-            scores = jnp.concatenate(
-                [
-                    jnp.where(key_scale <= own_column, scores[:, :fines], -jnp.inf),
-                    scores[:, fines:],
-                ],
+            pass_near(block, kv.at[:, coarse_rows(1, at)], chips + 1 + index)
+        flip(half, share)
+        for step, source in enumerate(order):
+            wait_bytes(kv.at[:, fine_rows(1, source)], near_recv.at[step])
+        flip(share, share + half)
+        for step, source in enumerate(order):
+            wait_bytes(kv.at[:, coarse_rows(1, source)], near_recv.at[chips + step])
+        flip(share + half, CORES * share)
+
+        def scales_of(owner):
+            return jnp.concatenate(
+                [scale_row[:, block_of(at * CORES + owner, rows)] for at in range(chips)], axis=1
+            )
+
+        key_scales = (scales_of(core), scales_of(1 - core))
+        groups = [range(low, low + 2) for low in range(0, chips, 2)]
+        for turn, group in enumerate(groups):
+            last = turn + 1 == len(groups)
+            for index in group:
+                if index:
+                    wait_bytes(qg.at[:, block_of(order[index], rows)], qg_recv.at[order[index]])
+            query, grad = [
+                jnp.concatenate([qg[slot, block_of(order[index], rows)] for index in group])
+                for slot in range(2)
+            ]
+            own_scale = jnp.concatenate(
+                [scale_row[:, block_of(order[index] * CORES + core, rows)] for index in group],
                 axis=1,
             )
+            own_column = jnp.transpose(
+                jnp.broadcast_to(own_scale, (HEAD, len(group) * rows))
+            )[:, :1]
+            scores = nn(query, flipped[0])
+            pieces = []
+            for part in range(CORES):
+                low = part * share
+                pieces += [
+                    jnp.where(
+                        key_scales[part] <= own_column, scores[:, low : low + half], -jnp.inf
+                    ),
+                    scores[:, low + half : low + share],
+                ]
+            scores = jnp.concatenate(pieces, axis=1)
+            dots = nn(grad, flipped[1])
             peak = jnp.max(scores, axis=1, keepdims=True)
-            powers = jnp.exp((scores - peak) * INVERSE)
+            powers = jnp.exp2((scores - peak) * (INVERSE * LOG2E))
             scale = 1.0 / jnp.sum(powers, axis=1, keepdims=True)
-            weights = powers * scale
-            dots = nt(grad, kv[1])
-            delta = jnp.sum(weights * dots, axis=1, keepdims=True)
-            weights = weights.astype(jnp.bfloat16)
-            grads = (weights.astype(jnp.float32) * (dots - delta) * INVERSE).astype(jnp.bfloat16)
-            out = nn(weights, kv[1]).astype(jnp.bfloat16)
-            query_out = nn(grads, kv[0]).astype(jnp.bfloat16)
-            for slot, value in enumerate((out, query_out)):
-                if not index:
-                    outs[slot][0, :, columns] = value
+            delta = jnp.sum(powers * dots, axis=1, keepdims=True) * scale
+            slope = scale * INVERSE
+            powers = powers.astype(jnp.bfloat16)
+            grads = powers * (dots - delta).astype(jnp.bfloat16)
+            sides = ((grads, query, slope), (powers, grad, scale))
+            for slot in (1, 0):
+                right_side, rows_in, factor = sides[slot]
+                scaled = (rows_in.astype(jnp.float32) * factor).astype(jnp.bfloat16)
+                value = nn(jnp.transpose(scaled), right_side)
+                if turn:
+                    value += accs[slot][...]
+                if not last:
+                    accs[slot][...] = value
                     continue
-                stage[slot, index - 1] = value
+                swap_out[slot] = value[:, share:].astype(jnp.bfloat16)
                 remote(
-                    stage.at[slot, index - 1],
-                    outs[slot].at[0, :, columns],
-                    row_send.at[slot, index - 1],
-                    out_recv.at[slot, unit],
+                    swap_out.at[slot],
+                    swap_in.at[slot],
+                    swap_send.at[slot],
+                    swap_recv.at[slot],
+                    partner,
+                )
+                accs[slot][:, :share] = value[:, :share]
+            for slot, (left_side, factor) in enumerate(((powers, scale), (grads, slope))):
+                value = (nn(left_side, kv[1 - slot]) * factor).astype(jnp.bfloat16)
+                for step, index in enumerate(group):
+                    block = value[step * rows : (step + 1) * rows]
+                    if not index:
+                        outs[slot][0, :, columns] = block
+                        continue
+                    stage[slot, index - 1] = block
+                    remote(
+                        stage.at[slot, index - 1],
+                        outs[slot].at[0, :, columns],
+                        row_send.at[slot, index - 1],
+                        out_recv.at[slot, unit],
+                        {"fine": order[index] * CORES + core},
+                    )
+
+        def give(slot, index, at):
+            for to_sub, to_dp in plane + [(sub, dp)]:
+                piece = (at * n_sub + to_sub) * n_dp + to_dp
+                src = total_out.at[slot, pl.ds(pl.multiple_of(half + piece * mine, mine), mine)]
+                dst = coarse_outs[slot].at[dp, :, head_columns(sub * heads + unit)]
+                if index == 0 and to_sub is sub and to_dp is dp:
+                    pltpu.make_async_copy(src, dst, coarse_recv.at[slot]).start()
+                else:
+                    remote(
+                        src,
+                        dst,
+                        coarse_send.at[slot],
+                        coarse_recv.at[slot],
+                        (at * CORES + core, to_sub, to_dp),
+                    )
+            block = total_out.at[slot, block_of(at, rows)]
+            result = outs[2 + slot]
+            if index:
+                remote(
+                    block,
+                    result.at[0, :, columns],
+                    key_send.at[slot, index - 1],
+                    out_recv.at[2 + slot, unit],
                     {"fine": at * CORES + core},
                 )
-            value_part, key_part = tn(weights, grad), tn(grads, query)
-            if index:
-                value_part += value_acc[...]
-                key_part += key_acc[...]
-            value_acc[...] = value_part
-            key_acc[...] = key_part
-
-        accs = (key_acc, value_acc)
-        for slot in (1, 0):
-            swap_out[slot, :half] = accs[slot][block_of(1 - core, half)].astype(jnp.bfloat16)
-            swap_out[slot, half:] = accs[slot][
-                pl.ds(pl.multiple_of(fines + (1 - core) * chalf, chalf), chalf)
-            ].astype(jnp.bfloat16)
-            remote(
-                swap_out.at[slot], swap_in.at[slot], swap_send.at[slot], swap_recv.at[slot], partner
-            )
+            else:
+                result[0, :, columns] = block[...]
+
         for slot in (1, 0):
             wait_bytes(swap_in.at[slot], swap_recv.at[slot])
-            total_out[slot, :half] = (
-                accs[slot][block_of(core, half)] + swap_in[slot, :half].astype(jnp.float32)
-            ).astype(jnp.bfloat16)
-            total_out[slot, half:] = (
-                accs[slot][pl.ds(pl.multiple_of(fines + core * chalf, chalf), chalf)]
-                + swap_in[slot, half:].astype(jnp.float32)
-            ).astype(jnp.bfloat16)
-            result = outs[2 + slot]
-            for index, at in reversed(list(enumerate(order))):
-                block = total_out.at[slot, block_of(at, rows)]
-                if index:
-                    remote(
-                        block,
-                        result.at[0, :, columns],
-                        key_send.at[slot, index - 1],
-                        out_recv.at[2 + slot, unit],
-                        {"fine": at * CORES + core},
-                    )
-                else:
-                    result[0, :, columns] = block[...]
-                for to_sub, to_dp in [(sub, dp)] + plane:
-                    piece = (at * n_sub + to_sub) * n_dp + to_dp
-                    src = total_out.at[
-                        slot, pl.ds(pl.multiple_of(half + piece * mine, mine), mine)
-                    ]
-                    dst = coarse_outs[slot].at[dp, :, head_columns(sub * heads + unit)]
-                    if index == 0 and to_sub is sub and to_dp is dp:
-                        pltpu.make_async_copy(src, dst, coarse_recv.at[slot]).start()
-                    else:
-                        remote(
-                            src,
-                            dst,
-                            coarse_send.at[slot],
-                            coarse_recv.at[slot],
-                            (at * CORES + core, to_sub, to_dp),
-                        )
+            total_out[slot] = jnp.transpose(
+                (accs[slot][:, :share] + swap_in[slot].astype(jnp.float32)).astype(jnp.bfloat16)
+            )
+            if chips > CORES:
+                give(slot, 1, given[0])
+        for index, at in list(enumerate(given))[1 if chips > CORES else 0 :]:
+            for slot in (1, 0):
+                give(slot, index + 1, at)
+        for slot in (1, 0):
+            give(slot, 0, chip)
 
     for head in range(heads):
 
@@ -813,13 +842,13 @@
     def _():
         for index in range(chips):
             wait_bytes(kv.at[:, :rows], near_send.at[index])
-            wait_bytes(kv.at[:, fines : fines + crows], near_send.at[chips + index])
+            wait_bytes(kv.at[:, half : half + crows], near_send.at[chips + index])
         for slot in range(2):
             wait_bytes(swap_out.at[slot], swap_send.at[slot])
             for index in range(chips - 1):
                 wait_bytes(stage.at[slot, index], row_send.at[slot, index])
                 wait_bytes(total_out.at[slot, :rows], key_send.at[slot, index])
-            wait_bytes(total_out.at[slot, : chalf - mine], coarse_send.at[slot])
+            wait_bytes(total_out.at[slot, : chips * crows - mine], coarse_send.at[slot])
 
 
 def fits_hosts(sizes, queries):
@@ -832,8 +861,8 @@
     rows, width = queries.shape[1:]
     heads, chips, mine = width // HEAD, n_fine // CORES, coarse_keys.shape[1]
     crows = mine * n_sub * n_dp
-    half = chips * (rows + crows)
-    total = CORES * half
+    share = chips * (rows + crows)
+    total = CORES * share
     bf16, f32 = jnp.bfloat16, jnp.float32
     dma = pltpu.SemaphoreType.DMA
     return pl.pallas_call(
@@ -849,13 +878,14 @@
             pltpu.VMEM((2,) + coarse_keys.shape, bf16),
             pltpu.VMEM((2, crows, width), bf16),
             pltpu.VMEM((2, total, HEAD), bf16),
+            pltpu.VMEM((2, HEAD, total), bf16),
             pltpu.VMEM((2, chips * rows, HEAD), bf16),
             pltpu.VMEM((2, chips - 1, rows, HEAD), bf16),
-            pltpu.VMEM((total, HEAD), f32),
-            pltpu.VMEM((total, HEAD), f32),
-            pltpu.VMEM((2, half, HEAD), bf16),
-            pltpu.VMEM((2, half, HEAD), bf16),
-            pltpu.VMEM((2, half, HEAD), bf16),
+            pltpu.VMEM((HEAD, total), f32),
+            pltpu.VMEM((HEAD, total), f32),
+            pltpu.VMEM((2, HEAD, share), bf16),
+            pltpu.VMEM((2, HEAD, share), bf16),
+            pltpu.VMEM((2, share, HEAD), bf16),
             dma((9,)),
             dma((4,)),
             dma,

time: 28.4 us -> 27.3 us (0.961)
  Pallas kernels: 27.6 us -> 26.5 us
    pallas_call x1, Pallas kernels: 26.9 us -> 25.8 us  [hosted(): pl.pallas_call(functools.partial(host_kernel, sizes), out_shape=[jax.Shap...]
where the time goes in v2:
time: 27.3 us; the launch traced here: 27.2 us
  Pallas kernels  26.5 us (97%)
  between operations  0.64 us (2%)
    pallas_call x1, Pallas kernels, hosted(): pl.pallas_call(functools.partial(host_kernel, sizes), out_shape=[jax.Shap...  25.8 us
    pallas_call x1, Pallas kernels, placed_out(): pl.pallas_call(functools.partial(place, count), out_shape=[jax.ShapeDtype...  0.77 us

profile of v2, /device:TPU:0, one launch (start us, length us, event | category | flops | bytes accessed | tf_op | source)
XLA Modules:
  0.0 27.2 jit_solution(1304283776787413675)
XLA Ops:
  0.6 25.8 %shard_map.118 = (bf16[1,128,256]{2,1,0:T(8,128)(2,1)S(1)}, bf16[1,128,256]{2,1,0:T(8,128)(2,1)S(1)}, bf16[1,128,256]{2,1,0:T(8,128)(2,1)S(1)}, bf16[1,128,256]{...) custom-call(bf16[1,128,256]{2,1,0:T(8,128)(2,1)} %queries.1, ...), custom_call_target="tpu_custom_call" | custom-call | tf_op jit(solution)/shard_map/pallas_call | solution.py:868
  26.4 0.8 %shard_map.119 = (bf16[1,128,256]{2,1,0:T(8,128)(2,1)}, bf16[1,128,256]{2,1,0:T(8,128)(2,1)}, bf16[1,128,256]{2,1,0:T(8,128)(2,1)}, bf16[1,128,256]{2,1,0:T(8,12...) custom-call(bf16[1,128,256]{2,1,0:T(8,128)(2,1)S(1)} %get-tuple-element.12.refs_0_, ...), custom_call_target="tpu_custom_call" | custom-call | tf_op jit(solution)/shard_map/pallas_call | solution.py:941
